TPU v7x, 32 devices: a whole 2x2x4 slice. The times are simulated.
32 devices in a mesh: grp: 4 (over x, core), row: 4 (over z), col: 2 (over y).
Axes of the slice: x: 2, y: 2, z: 4, core: 2. Of those that a mesh axis runs over, the one named last changes fastest.
Arguments:
- fields: bfloat16 [4, 4, 192, 1536], P('grp', None, 'row', 'col'), may hold values from -12 to 12
- offset: int32 [1], replicated, may hold values from 0 to 191
- level_index: int32 [4], replicated, may hold values from 0 to 3, each once
- nudge_rate: float32 [4], replicated, may hold values from 0.2 to 0.9
- driving: float32 [4, 64, 64], replicated, may hold values from -4 to 4
Outputs:
- nudged: bfloat16 [4, 4, 192, 1536], P('grp', None, 'row', 'col')
Inputs may be any that keep to these rules, and one draw needn't show every extreme that they name: `offset`: the footprint covers a third of the parent rows from there on, wrapping around the periodic domain. `level_index`: each parent level is fed by exactly one child level.
All inputs are finite; a program needn't handle non-finite values.
Results may differ from a plain program's by a relative error of at most 0.0034.
Values may be sent and summed in bfloat16 or wider, within the bound.
No kernel may reach another device: no remote copies, remote signals or barrier semaphores. Data moves between devices by JAX's collectives and lax.ppermute only.
A program may use at most 64 MiB of HBM per device.

v0:
```python
import math
import jax
import jax.numpy as jnp
from jax import lax
from jax.sharding import PartitionSpec as P

MAX_WAVE = 32


def from_root(block, axis, source):
    block = jnp.where(lax.axis_index(axis) == source, block, jnp.zeros_like(block))
    return lax.psum(block, axis)


def fourier_table(positions, cell_count, max_order):
    orders = jnp.arange(1, max_order + 1, dtype=jnp.int32)
    period = 3 * cell_count
    phase_index = positions[:, None] * orders[None, :] % period
    angles = phase_index.astype(jnp.float32) * jnp.float32(2.0 * math.pi / period)
    wave_scale = jnp.float32(math.sqrt(2.0 / cell_count))
    constant = jnp.full((positions.shape[0], 1), 1.0 / math.sqrt(cell_count), jnp.float32)
    return jnp.concatenate(
        [constant, wave_scale * jnp.cos(angles), wave_scale * jnp.sin(angles[:, : max_order - 1])],
        axis=1,
    )


def place_rows(carried, block_rows, strip_index):
    height = block_rows.shape[1]
    inside = (strip_index >= 0) & (strip_index < height)
    picked = jnp.take(block_rows, jnp.clip(strip_index, 0, height - 1), axis=1)
    mask_shape = (1, inside.shape[0]) + (1,) * (block_rows.ndim - 2)
    return jnp.where(inside.reshape(mask_shape), picked, carried)


def per_device(fields, offset, level_index, nudge_rate, driving):
    group_id = lax.axis_index("grp")
    row_id = lax.axis_index("row")
    col_id = lax.axis_index("col")
    group_count = lax.axis_size("grp")
    local_slab = fields[0]
    levels, tile_rows, tile_cols = local_slab.shape
    full_rows = lax.axis_size("row") * tile_rows
    full_cols = lax.axis_size("col") * tile_cols
    third_rows = tile_rows // 3
    third_cols = tile_cols // 3
    shift_rows = offset[0]
    is_parent = group_id == group_count - 1
    level_ids = jnp.arange(levels, dtype=jnp.int32)
    inverse = jnp.sum(
        level_ids[:, None] * (level_index[:, None] == level_ids[None, :]).astype(jnp.int32), axis=0
    )
    parent_rows = row_id * tile_rows + jnp.arange(tile_rows, dtype=jnp.int32)
    parent_cols = col_id * tile_cols + jnp.arange(tile_cols, dtype=jnp.int32)
    strip_index = (parent_rows - shift_rows) % full_rows
    covered = strip_index < full_rows // 3
    row_table = fourier_table(3 * parent_rows, full_rows, MAX_WAVE)
    col_table = fourier_table(3 * parent_cols, full_cols, MAX_WAVE)
    row_half = lax.optimization_barrier(row_table.astype(jnp.bfloat16))
    row_rounded = row_half.astype(jnp.float32)
    col_rounded = col_table.astype(jnp.bfloat16)
    block_sums = jnp.sum(
        local_slab.reshape(levels, third_rows, 3, third_cols, 3), axis=(2, 4), dtype=jnp.float32
    )
    averaged = (block_sums / 9.0).astype(jnp.bfloat16)
    by_parent = jnp.take(averaged, inverse, axis=0)
    empty_tile = jnp.zeros((levels, tile_rows, third_cols), jnp.bfloat16)
    placed = place_rows(
        empty_tile, lax.all_gather(by_parent, "row", axis=1, tiled=True), strip_index
    )
    thirds = lax.all_gather(placed[:, :, None, :], "grp", axis=2, tiled=True)
    arrived = thirds[:, :, : group_count - 1, :].reshape(levels, tile_rows, tile_cols)
    fed_tile = jnp.where(covered[None, :, None], arrived, local_slab)
    projected = jnp.einsum("lrc,cm->lrm", fed_tile, col_rounded, preferred_element_type=jnp.float32)
    partial_sums = jnp.einsum(
        "rn,lrm->lnm", row_rounded, projected, precision=lax.Precision.HIGHEST
    )
    summed = lax.psum(partial_sums, ("row", "col"))
    coeffs = from_root(summed, "grp", group_count - 1)
    amplitude = math.sqrt(full_rows * full_cols) / (2 * MAX_WAVE)
    deficit = amplitude * driving - coeffs
    child_rows = (3 * shift_rows + parent_rows - 1) % (3 * full_rows)
    child_cols = (
        (3 * col_id + group_id) * tile_cols + jnp.arange(tile_cols, dtype=jnp.int32) - 1
    ) % (3 * full_cols)
    rows_used = jnp.where(is_parent, row_table, fourier_table(child_rows, full_rows, MAX_WAVE))
    cols_used = jnp.where(is_parent, col_table, fourier_table(child_cols, full_cols, MAX_WAVE))
    level_deficit = jnp.where(is_parent, deficit, jnp.take(deficit, level_index, axis=0))
    level_rate = jnp.where(is_parent, nudge_rate, jnp.take(nudge_rate, level_index, axis=0))
    base_tile = jnp.where(is_parent, fed_tile, local_slab)
    spread_cols = jnp.einsum(
        "lnm,cm->lnc", level_deficit, cols_used, precision=lax.Precision.HIGHEST
    )
    increment = jnp.einsum("rn,lnc->lrc", rows_used, spread_cols, precision=lax.Precision.HIGHEST)
    result = (base_tile.astype(jnp.float32) + level_rate[:, None, None] * increment).astype(
        jnp.bfloat16
    )
    return result[None]


def solution(mesh):
    placed = (P("grp", None, "row", "col"), P(), P(), P(), P())
    return jax.shard_map(
        per_device,
        mesh=mesh,
        in_specs=placed,
        out_specs=P("grp", None, "row", "col"),
        check_vma=False,
    )
```

profile of v0, /device:TPU:0, one launch (start us, length us, event | category | flops | bytes accessed | tf_op | source)
XLA Modules:
  0.0 187.4 jit_solution(7154075441931077724)
XLA Ops:
  6.5 0.0 all-reduce.3.cloned.1.call-start
  6.5 0.7 select_reduce_fusion
  8.0 0.0 copy-start.1
  8.0 0.0 copy-start.3
  8.0 0.0 copy-start
  8.0 0.0 copy-start.2
  8.1 25.9 %reshape.136 = f32[4,16,3,256,3]{4,3,2,1,0:T(8,128)} reshape(bf16[1,4,48,768]{3,2,1,0:T(8,128)(2,1)} %param.5) | data formatting | bytes 884736 | tf_op jit(solution)/shard_map/convert_element_type | solution.py:62
  34.0 11.8 %reduce_sum.21 = f32[4,16,256]{2,1,0:T(8,128)S(1)} reduce(f32[4,16,3,256,3]{4,3,2,1,0:T(8,128)} %reshape.136, f32[]{:T(128)} %constant.140.clone.1), dimensions={2,4}, to_apply=%region_1.2 | reduce | flops 131072 | bytes 655364 | tf_op jit(solution)/shard_map/reduce_sum | solution.py:62
  45.8 0.5 gather_fusion
  46.3 0.1 broadcast_select_fusion.1
  46.4 15.1 %all_gather.6 = bf16[4,64,256]{2,1,0:T(8,128)(2,1)S(1)} all-gather(bf16[4,16,256]{2,1,0:T(8,128)(2,1)S(1)} %broadcast_select_fusion.1), channel_id=1, replica_groups=mesh['grp'=4,'row'=4,'col'=2] {'row'}, dimensions={1}, use_global_device_ids=true | all-gather | bytes 163840 | tf_op jit(solution)/shard_map/all_gather | solution.py:69
  61.5 0.1 copy.20
  61.6 0.7 gather_fusion.1
  62.3 0.1 fusion.24
  62.4 6.5 %all_gather.7 = bf16[4,48,4,256]{3,1,0,2:T(8,128)(2,1)S(1)} all-gather(bf16[4,48,1,256]{3,1,0,2:T(8,128)(2,1)S(1)} %fusion.24), channel_id=1, replica_groups=mesh['grp'=4,'row'=4,'col'=2] {'grp'}, dimensions={2}, use_global_device_ids=true | all-gather | bytes 491520 | tf_op jit(solution)/shard_map/all_gather | solution.py:71
  68.9 0.8 cosine_multiply_fusion.1
  69.7 0.3 fusion.21
  70.1 0.3 cosine_multiply_fusion.2
  70.4 0.1 fusion.40
  70.5 0.1 fusion.55
  70.6 0.0 copy-done.1
  70.6 0.3 fusion.13
  70.9 1.0 convolution_bitcast_fusion
  71.9 0.0 all-reduce.3.cloned.1.call-update
  71.9 0.0 all-reduce.5.cloned.1.call-start
  71.9 0.0 copy-done.3
  72.0 0.3 fusion.20
  72.3 0.1 fusion.39
  72.4 0.0 copy-done
  72.4 0.6 gather_fusion.2
  73.1 70.4 %all-reduce.3.cloned.1.call-done = f32[4,64,64]{1,2,0:T(8,128)} async-done(((f32[4,64,64]{1,2,0:T(8,128)}), f32[4,64,64]{1,2,0:T(8,128)}) %all-reduce.3.cloned.1.call-update) | async-done | bytes 65552 | tf_op jit(solution)/shard_map/psum | solution.py:78
  143.4 0.7 broadcast_select_fusion
  144.1 0.0 all-reduce.5.cloned.1.call-update
  144.1 0.0 copy-done.2
  144.1 0.1 copy.23
  144.2 32.4 %all-reduce.5.cloned.1.call-done = f32[4,64,64]{1,2,0:T(8,128)} async-done(((f32[4,64,64]{1,2,0:T(8,128)}), f32[4,64,64]{1,2,0:T(8,128)}) %all-reduce.5.cloned.1.call-update) | async-done | bytes 65552 | tf_op jit(solution)/shard_map/psum | solution.py:12
  176.6 0.9 multiply_subtract_fusion
  177.6 0.6 gather_fusion.3
  178.1 0.9 fusion.5
  179.1 1.5 fusion.3
  (19 shorter events, 0.2 us)
Async XLA Ops:
  6.5 136.9 %all-reduce.3.cloned.1.call-start = ((), (), s32[]{:S(2)}) async-start(), calls=%async_computation | async-start | bytes 262144 | tf_op jit(solution)/shard_map/psum | solution.py:78
  8.0 62.6 %copy-start.1 = (bf16[1,4,48,768]{3,2,1,0:T(8,128)(2,1)S(1)}, bf16[1,4,48,768]{3,2,1,0:T(8,128)(2,1)}, u32[]{:S(2)}) copy-start(bf16[1,4,48,768]{3,2,1,0:T(8,128)(2,1)} %param.5) | copy-start | bytes 884740
  8.0 63.9 %copy-start.3 = (s32[4]{0:T(128)S(1)}, s32[4]{0:T(128)}, u32[]{:S(2)}) copy-start(s32[4]{0:T(128)} %param.7) | copy-start | bytes 52
  8.0 64.4 %copy-start = (f32[4]{0:T(128)S(1)}, f32[4]{0:T(128)}, u32[]{:S(2)}) copy-start(f32[4]{0:T(128)} %param.8) | copy-start | bytes 52
  8.0 136.1 %copy-start.2 = (f32[4,64,64]{2,1,0:T(8,128)S(1)}, f32[4,64,64]{2,1,0:T(8,128)}, u32[]{:S(2)}) copy-start(f32[4,64,64]{2,1,0:T(8,128)} %param.9) | copy-start | bytes 196612
  71.9 104.8 %all-reduce.5.cloned.1.call-start = ((), (), s32[]{:S(2)}) async-start(), calls=%async_computation.1 | async-start | bytes 262144 | tf_op jit(solution)/shard_map/psum | solution.py:12
Sparse Core Ops, SparseCore 0:
  72.0 71.3 all-reduce.2
  145.7 30.8 all-reduce.4
where the time goes:
time: 188 us; the launch traced here: 187 us
  waiting for transfers between devices  103 us (55%)
  local copies, waits for them, and re-layouts  28.6 us (15%)
  blocking collectives  21.5 us (11%)
  other arithmetic  16.5 us (9%)
  between operations  14.3 us (8%)
  matrix products  3.65 us (2%)
    psum x1, waiting for transfers between devices, per_device(): summed = lax.psum(partial_sums, ('row', 'col'))  70.4 us
    psum x1, waiting for transfers between devices, from_root(): return lax.psum(block, axis)  32.4 us
    convert_element_type x1, local copies, waits for them, and re-layouts, per_device(): jnp.sum(local_slab.reshape(levels, third_rows, 3, third_cols, 3), axis=(2...  25.9 us
    all_gather x1, blocking collectives, per_device(): lax.all_gather(by_parent, 'row', axis=1, tiled=True)  15.1 us
    reduce_sum x1, other arithmetic, per_device(): jnp.sum(local_slab.reshape(levels, third_rows, 3, third_cols, 3), axis=(2...  11.8 us
    all_gather x1, blocking collectives, per_device(): thirds = lax.all_gather(placed[:, :, None, :], 'grp', axis=2, tiled=True)  6.46 us
  transfers between devices with their start and end apart: 2, of which 2 were waited for; matrix products, arithmetic and copies ran while one was open for 1% of the time, Pallas kernels for 0%

commit v1 on v0

--- a/solution.py
+++ b/solution.py
@@ -7,9 +7,15 @@
 MAX_WAVE = 32
 
 
+def add_all(x, mesh_axis):
+    parts = lax.all_gather(x, mesh_axis, axis=0, tiled=False)
+    summed = parts.sum(axis=0)
+    return summed
+
+
 def from_root(block, axis, source):
     block = jnp.where(lax.axis_index(axis) == source, block, jnp.zeros_like(block))
-    return lax.psum(block, axis)
+    return add_all(block, axis)
 
 
 def fourier_table(positions, cell_count, max_order):

time: 188 us -> 161 us (0.86)
  waiting for transfers between devices: 103 us -> 70.3 us
  blocking collectives: 21.5 us -> 28.7 us
    psum x1 -> x0, waiting for transfers between devices: 32.4 us -> none  [from_root(): return lax.psum(block, axis)]
    all_gather x0 -> x1, blocking collectives: none -> 7.15 us  [add_all(): parts = lax.all_gather(x, mesh_axis, axis=0, tiled=False)]
  transfers between devices with their start and end apart: 2 -> 1, of which waited for: 2 -> 1; matrix products, arithmetic and copies ran while one was open for 1% -> 1% of each run, Pallas kernels for 0% -> 0%
where the time goes in v1:
time: 161 us
  waiting for transfers between devices  70.3 us (44%)
  local copies, waits for them, and re-layouts  28.8 us (18%)
  blocking collectives  28.7 us (18%)
  other arithmetic  14.9 us (9%)
  between operations  14.3 us (9%)
  matrix products  3.66 us (2%)
    psum x1, waiting for transfers between devices, per_device(): summed = lax.psum(partial_sums, ('row', 'col'))  70.3 us
    convert_element_type x1, local copies, waits for them, and re-layouts, per_device(): jnp.sum(local_slab.reshape(levels, third_rows, 3, third_cols, 3), axis=(2...  25.9 us
    all_gather x1, blocking collectives, per_device(): lax.all_gather(by_parent, 'row', axis=1, tiled=True)  15.1 us
    reduce_sum x1, other arithmetic, per_device(): jnp.sum(local_slab.reshape(levels, third_rows, 3, third_cols, 3), axis=(2...  11.8 us
    all_gather x1, blocking collectives, add_all(): parts = lax.all_gather(x, mesh_axis, axis=0, tiled=False)  7.15 us
    all_gather x1, blocking collectives, per_device(): thirds = lax.all_gather(placed[:, :, None, :], 'grp', axis=2, tiled=True)  6.46 us
  transfers between devices with their start and end apart: 1, of which 1 were waited for; matrix products, arithmetic and copies ran while one was open for 1% of the time, Pallas kernels for 0%

profile of v1, /device:TPU:0, one launch (start us, length us, event | category | flops | bytes accessed | tf_op | source)
XLA Modules:
  0.0 160.7 jit_solution(10720829274543634851)
XLA Ops:
  6.5 0.0 all-reduce.2.cloned.1.call-start
  6.5 0.7 select_reduce_fusion
  8.0 0.0 copy-start.1
  8.0 0.0 copy-start.3
  8.0 0.0 copy-start
  8.0 0.0 copy-start.2
  8.1 25.9 %reshape.136 = f32[4,16,3,256,3]{4,3,2,1,0:T(8,128)} reshape(bf16[1,4,48,768]{3,2,1,0:T(8,128)(2,1)} %param.5) | data formatting | bytes 884736 | tf_op jit(solution)/shard_map/convert_element_type | solution.py:68
  34.0 11.8 %reduce_sum.30 = f32[4,16,256]{2,1,0:T(8,128)S(1)} reduce(f32[4,16,3,256,3]{4,3,2,1,0:T(8,128)} %reshape.136, f32[]{:T(128)} %constant.140.clone.1), dimensions={2,4}, to_apply=%region_1.2 | reduce | flops 131072 | bytes 655364 | tf_op jit(solution)/shard_map/reduce_sum | solution.py:68
  45.8 0.5 gather_fusion
  46.3 0.1 broadcast_select_fusion.1
  46.4 15.1 %all_gather.12 = bf16[4,64,256]{2,1,0:T(8,128)(2,1)S(1)} all-gather(bf16[4,16,256]{2,1,0:T(8,128)(2,1)S(1)} %broadcast_select_fusion.1), channel_id=1, replica_groups=mesh['grp'=4,'row'=4,'col'=2] {'row'}, dimensions={1}, use_global_device_ids=true | all-gather | bytes 163840 | tf_op jit(solution)/shard_map/all_gather | solution.py:75
  61.5 0.1 copy.28
  61.6 0.7 gather_fusion.1
  62.3 0.1 fusion.24
  62.4 6.5 %all_gather.13 = bf16[4,48,4,256]{3,1,0,2:T(8,128)(2,1)S(1)} all-gather(bf16[4,48,1,256]{3,1,0,2:T(8,128)(2,1)S(1)} %fusion.24), channel_id=1, replica_groups=mesh['grp'=4,'row'=4,'col'=2] {'grp'}, dimensions={2}, use_global_device_ids=true | all-gather | bytes 491520 | tf_op jit(solution)/shard_map/all_gather | solution.py:77
  68.9 0.8 cosine_multiply_fusion.1
  69.7 0.3 fusion.21
  70.1 0.3 cosine_multiply_fusion.2
  70.4 0.1 fusion.40
  70.5 0.1 fusion.55
  70.6 0.0 copy-done.1
  70.6 0.3 fusion.13
  70.9 1.0 convolution_bitcast_fusion
  71.9 0.0 all-reduce.2.cloned.1.call-update
  71.9 0.0 copy-done.3
  71.9 0.3 fusion.20
  72.3 0.1 fusion.39
  72.4 0.0 copy-done
  72.4 0.6 gather_fusion.2
  73.0 0.0 copy-done.2
  73.0 0.1 copy.31
  73.1 70.3 %all-reduce.2.cloned.1.call-done = f32[4,64,64]{1,2,0:T(8,128)} async-done(((f32[4,64,64]{1,2,0:T(8,128)}), f32[4,64,64]{1,2,0:T(8,128)}) %all-reduce.2.cloned.1.call-update) | async-done | bytes 65552 | tf_op jit(solution)/shard_map/psum | solution.py:84
  143.5 0.1 copy.32
  143.6 7.1 %all-gather = f32[16,64,64]{2,1,0:T(8,128)S(1)} all-gather(f32[4,64,64]{2,1,0:T(8,128)S(1)} %copy.32), channel_id=2, replica_groups=mesh['grp'=4,'row'=4,'col'=2] {'grp'}, dimensions={0}, use_global_device_ids=true | all-gather | bytes 327680 | tf_op jit(solution)/shard_map/all_gather | solution.py:11
  150.8 0.1 copy.33
  150.9 0.6 gather_fusion.3
  151.5 0.9 fusion.5
  152.4 1.5 fusion.3
  (22 shorter events, 0.3 us)
Async XLA Ops:
  6.5 136.9 %all-reduce.2.cloned.1.call-start = ((), (), s32[]{:S(2)}) async-start(), calls=%async_computation | async-start | bytes 262144 | tf_op jit(solution)/shard_map/psum | solution.py:84
  8.0 62.6 %copy-start.1 = (bf16[1,4,48,768]{3,2,1,0:T(8,128)(2,1)S(1)}, bf16[1,4,48,768]{3,2,1,0:T(8,128)(2,1)}, u32[]{:S(2)}) copy-start(bf16[1,4,48,768]{3,2,1,0:T(8,128)(2,1)} %param.5) | copy-start | bytes 884740
  8.0 63.9 %copy-start.3 = (s32[4]{0:T(128)S(1)}, s32[4]{0:T(128)}, u32[]{:S(2)}) copy-start(s32[4]{0:T(128)} %param.7) | copy-start | bytes 52
  8.0 64.3 %copy-start = (f32[4]{0:T(128)S(1)}, f32[4]{0:T(128)}, u32[]{:S(2)}) copy-start(f32[4]{0:T(128)} %param.8) | copy-start | bytes 52
  8.0 65.0 %copy-start.2 = (f32[4,64,64]{2,1,0:T(8,128)S(1)}, f32[4,64,64]{2,1,0:T(8,128)}, u32[]{:S(2)}) copy-start(f32[4,64,64]{2,1,0:T(8,128)} %param.9) | copy-start | bytes 196612
Sparse Core Ops, SparseCore 0:
  72.0 71.4 all-reduce.1
